TPU v7x, 16 devices: a whole 2x2x2 slice. The times are simulated.
16 devices in a mesh: dp: 2 (over z), tp: 8 (over y, x, core).
Axes of the slice: x: 2, y: 2, z: 2, core: 2. Of those that a mesh axis runs over, the one named last changes fastest.
Arguments:
- hidden: bfloat16 [6, 512, 960], P('dp')
- norm_w: bfloat16 [960], replicated
- embed_table: bfloat16 [49152, 960], P('tp')
- labels: int32 [6, 512], P('dp')
- loss_mask: int32 [6, 512], P('dp')
Outputs:
- output 1: float32 [], replicated
- output 2: bfloat16 [6, 512, 960], P('dp')
- output 3: float32 [960], replicated
- output 4: float32 [49152, 960], P('tp')
All inputs are finite; a program needn't handle non-finite values.
Results may differ from a plain program's by a relative error of at most 0.001.
Values sent between devices are 32-bit elements.
A program may use at most 1 GiB of HBM per device.

v0:
```python
import jax
import jax.numpy as jnp
from jax import lax
from jax.sharding import PartitionSpec as P

SOFT_CAP = 30.0


def norm_apply(hid_rows, gain32):
    h32 = hid_rows.astype(jnp.float32)
    inv_rms = lax.rsqrt(jnp.mean(h32 * h32, axis=-1, keepdims=True) + 1e-6)
    return h32 * inv_rms * (1.0 + gain32)


def solution(mesh):
    def local_step(hidden, norm_w, embed_table, labels, loss_mask):
        batch_rows, seq_len, model_dim = hidden.shape
        vocab_local = embed_table.shape[0]
        tokens = batch_rows * seq_len
        hid_rows = hidden.reshape(tokens, model_dim)
        mask_rows = loss_mask.reshape(tokens).astype(jnp.float32)
        tok_count = jnp.maximum(lax.psum(jnp.sum(mask_rows), 'dp'), 1.0)
        normed, norm_back = jax.vjp(norm_apply, hid_rows, norm_w.astype(jnp.float32))
        normed_bf = normed.astype(jnp.bfloat16)
        logits = jnp.einsum('td,vd->tv', normed_bf, embed_table, preferred_element_type=jnp.float32)
        capped = SOFT_CAP * jnp.tanh(logits / SOFT_CAP)
        row_max = lax.pmax(jnp.max(capped, axis=-1), 'tp')
        exp_shift = jnp.exp(capped - row_max[:, None])
        row_sum = lax.psum(jnp.sum(exp_shift, axis=-1), 'tp')
        local_ids = labels.reshape(tokens) - lax.axis_index('tp') * vocab_local
        onehot = lax.broadcasted_iota(jnp.int32, (1, vocab_local), 1) == local_ids[:, None]
        picked = lax.psum(jnp.sum(jnp.where(onehot, capped, 0.0), axis=-1), 'tp')
        tok_loss = jnp.log(row_sum) + row_max - picked
        mean_loss = lax.psum(jnp.sum(mask_rows * tok_loss), 'dp') / tok_count
        tok_scale = mask_rows / tok_count
        cap_ratio = capped / SOFT_CAP
        grad_logit = ((exp_shift / row_sum[:, None] - onehot.astype(jnp.float32)) * tok_scale[:, None] * (1.0 - cap_ratio * cap_ratio)).astype(jnp.bfloat16)
        grad_part = jnp.einsum('tv,vd->td', grad_logit, embed_table, preferred_element_type=jnp.float32)
        grad_x = lax.psum(grad_part, 'tp')
        grad_rows, grad_gain = norm_back(grad_x)
        grad_gain = lax.psum(grad_gain, 'dp')
        table_part = jnp.einsum('tv,td->vd', grad_logit, normed_bf, preferred_element_type=jnp.float32)
        grad_table = lax.psum(table_part, 'dp')
        return mean_loss, grad_rows.reshape(batch_rows, seq_len, model_dim), grad_gain, grad_table

    return jax.shard_map(local_step, mesh=mesh, in_specs=(P('dp', None, None), P(None), P('tp', None), P('dp', None), P('dp', None)), out_specs=(P(), P('dp', None, None), P(None), P('tp', None)), check_vma=False)
```

profile of v0, /device:TPU:0, one launch (start us, length us, event | category | flops | bytes accessed | tf_op | source)
XLA Modules:
  0.0 814.9 jit_solution(15589512693866190265)
XLA Ops:
  7.2 0.0 copy-start.3
  7.2 0.0 copy-start.2
  7.2 0.0 all-reduce.5.cloned.1.call-start
  7.2 1.3 convert_reduce_fusion
  8.5 0.7 convert_element_type.35
  9.2 2.4 multiply_reduce_fusion.2
  11.7 5.3 copy.11
  17.0 6.8 psum.52
  23.8 0.0 copy-done.3
  23.8 0.0 copy-done.2
  23.9 0.0 copy-start
  23.9 6.6 copy.12
  30.5 31.8 %fusion.2 = (f32[1536]{0:T(1024)S(1)}, f32[1536,6144]{1,0:T(8,128)}) fusion(bf16[6144,960]{0,1:T(8,128)(2,1)} %param.7, f32[1536,960]{0,1:T(8,128)} %copy.12, f32[960]{0:T(1024)S(1)} %convert_add_fusion, f32[1536]{0:T(1024)S(1)} %rsqrt.10), kind=kOutput, calls=%fused_computation.7 | convolution fusion | flops 18152126464 | bytes 55459584 | tf_op jit(solution)/shard_map/td,vd->tv/dot_general | solution.py:25
  62.3 0.0 copy-done
  62.3 13.2 %pmax.7 = f32[1536]{0:T(1024)S(1)} all-reduce(f32[1536]{0:T(1024)S(1)} %get-tuple-element.22), channel_id=1, replica_groups=mesh['dp'=2,'tp'=8] {'tp'}, use_global_device_ids=true, to_apply=%region_2.0 | all-reduce | flops 1536 | bytes 12288 | tf_op jit(solution)/shard_map/pmax | solution.py:27
  76.2 23.4 %fusion.1 = (f32[1536]{0:T(1024)S(1)}, f32[1536]{0:T(1024)S(1)}) fusion(f32[1536,6144]{1,0:T(8,128)} %get-tuple-element.23, f32[1536]{0:T(1024)S(1)} %pmax.7, s32[1536]{0:T(1024)S(1)} %sub.37), kind=kLoop, calls=%fused_computation.6 | loop fusion | flops 66057216 | bytes 37773312 | tf_op jit(solution)/shard_map/reduce_sum | solution.py:29
  99.5 22.5 %all-reduce = (f32[1536]{0:T(1024)S(1)}, f32[1536]{0:T(1024)S(1)}) all-reduce(f32[1536]{0:T(1024)S(1)} %get-tuple-element.13, f32[1536]{0:T(1024)S(1)} %get-tuple-element.12), channel_id=1, replica_groups=mesh['dp'=2,'tp'=8] {'tp'}, use_global_device_ids=true, to_apply=%region_6.0 | all-reduce | flops 3072 | bytes 24576 | tf_op jit(solution)/shard_map/psum | solution.py:32
  122.1 0.6 broadcast_divide_fusion
  122.7 27.7 %multiply_convert_fusion = bf16[1536,6144]{1,0:T(8,128)(2,1)} fusion(f32[1536,6144]{1,0:T(8,128)} %get-tuple-element.23, f32[1536]{0:T(1024)S(1)} %get-tuple-element.20, f32[1536]{0:T(1024)S(1)} %get-tuple-element.17, s32[1536]{0:T(1024)S(1)} %sub.37, f32[1536]{0:T(1024)S(1)} %pmax.7), kind=kLoop, calls=%fused_computation | loop fusion | flops 113246208 | bytes 56647680 | tf_op jit(solution)/shard_map/convert_element_type | solution.py:37
  150.4 24.9 %fusion.6 = f32[1536,960]{0,1:T(8,128)} fusion(bf16[1536,6144]{1,0:T(8,128)(2,1)} %multiply_convert_fusion, bf16[6144,960]{0,1:T(8,128)(2,1)} %param.7), kind=kOutput, calls=%fused_computation.23 | convolution fusion | flops 18119393280 | bytes 36569088 | tf_op jit(solution)/shard_map/tv,vd->td/dot_general | solution.py:38
  175.3 0.0 all-reduce.5.cloned.1.call-update
  175.4 0.0 all-reduce.7.cloned.1.call-start
  175.4 26.7 %fusion.4 = f32[6144,960]{0,1:T(8,128)} fusion(bf16[1536,6144]{1,0:T(8,128)(2,1)} %multiply_convert_fusion, f32[1536,960]{0,1:T(8,128)} %copy.12, f32[960]{0:T(1024)S(1)} %convert_add_fusion, f32[1536]{0:T(1024)S(1)} %rsqrt.10), kind=kOutput, calls=%fused_computation.21 | convolution fusion | flops 18123816960 | bytes 48375552 | tf_op jit(solution)/shard_map/tv,td->vd/dot_general | solution.py:42
  202.1 0.0 all-reduce.7.cloned.1.call-update
  202.1 0.0 copy-start.1
  202.1 64.7 %all-reduce.5.cloned.1.call-done = f32[1536,960]{0,1:T(8,128)} async-done(((f32[1536,960]{0,1:T(8,128)}), f32[1536,960]{0,1:T(8,128)}) %all-reduce.5.cloned.1.call-update) | async-done | bytes 5898256 | tf_op jit(solution)/shard_map/psum | solution.py:39
  266.8 5.9 multiply_reduce_fusion
  272.7 5.9 all-reduce.1
  279.2 0.0 copy-done.1
  279.2 7.1 fusion.3
  286.4 3.1 copy.15
  289.5 2.8 copy.16
  292.3 498.1 %all-reduce.7.cloned.1.call-done = f32[6144,960]{0,1:T(8,128)} async-done(((f32[6144,960]{0,1:T(8,128)}), f32[6144,960]{0,1:T(8,128)}) %all-reduce.7.cloned.1.call-update) | async-done | bytes 23592976 | tf_op jit(solution)/shard_map/psum | solution.py:43
  790.4 16.6 %copy.19 = f32[6144,960]{0,1:T(8,128)} copy(f32[6144,960]{0,1:T(8,128)} %all-reduce.7.cloned.1.call-done) | data formatting | bytes 47185920
  (8 shorter events, 0.1 us)
Async XLA Ops:
  7.2 16.7 %copy-start.3 = (bf16[960]{0:T(1024)(128)(2,1)S(1)}, bf16[960]{0:T(1024)(128)(2,1)}, u32[]{:S(2)}) copy-start(bf16[960]{0:T(1024)(128)(2,1)} %param.6) | copy-start | bytes 5764
  7.2 16.7 %copy-start.2 = (s32[3,512]{1,0:T(4,128)S(1)}, s32[3,512]{1,0:T(4,128)}, u32[]{:S(2)}) copy-start(s32[3,512]{1,0:T(4,128)} %param.8) | copy-start | bytes 18436
  7.2 259.6 %all-reduce.5.cloned.1.call-start = ((), (), s32[]{:S(2)}) async-start(), calls=%async_computation | async-start | bytes 11796480 | tf_op jit(solution)/shard_map/psum | solution.py:39
  23.9 38.5 %copy-start = (f32[1536]{0:T(1024)}, f32[1536]{0:T(1024)S(1)}, u32[]{:S(2)}) copy-start(f32[1536]{0:T(1024)S(1)} %add.41) | copy-start | bytes 18436
  175.4 615.0 %all-reduce.7.cloned.1.call-start = ((), (), s32[]{:S(2)}) async-start(), calls=%async_computation.1 | async-start | bytes 47185920 | tf_op jit(solution)/shard_map/psum | solution.py:43
  202.1 77.1 %copy-start.1 = (f32[1536]{0:T(1024)S(1)}, f32[1536]{0:T(1024)}, u32[]{:S(2)}) copy-start(f32[1536]{0:T(1024)} %copy-done) | copy-start | bytes 18436
Sparse Core Ops, SparseCore 0:
  175.5 91.2 all-reduce.4
  269.8 520.5 all-reduce.6
where the time goes:
time: 816 us; the launch traced here: 815 us
  waiting for transfers between devices  563 us (69%)
  matrix products  83.5 us (10%)
  other arithmetic  69.1 us (8%)
  blocking collectives  48.4 us (6%)
  local copies, waits for them, and re-layouts  34.5 us (4%)
  between operations  16.6 us (2%)
    psum x1, waiting for transfers between devices, local_step(): grad_table = lax.psum(table_part, 'dp')  498 us
    psum x1, waiting for transfers between devices, local_step(): grad_x = lax.psum(grad_part, 'tp')  64.7 us
    dot_general x1, matrix products, local_step(): jnp.einsum('td,vd->tv', normed_bf, embed_table, preferred_element_type=jn...  31.8 us
    convert_element_type x1, other arithmetic, local_step(): ((exp_shift / row_sum[:, None] - onehot.astype(jnp.float32)) * tok_scale[...  27.7 us
    dot_general x1, matrix products, local_step(): jnp.einsum('tv,td->vd', grad_logit, normed_bf, preferred_element_type=jnp...  26.7 us
    dot_general x1, matrix products, local_step(): jnp.einsum('tv,vd->td', grad_logit, embed_table, preferred_element_type=j...  24.9 us
    reduce_sum x1, other arithmetic, local_step(): row_sum = lax.psum(jnp.sum(exp_shift, axis=-1), 'tp')  23.4 us
    psum x1, blocking collectives, local_step(): picked = lax.psum(jnp.sum(jnp.where(onehot, capped, 0.0), axis=-1), 'tp')  22.5 us
  transfers between devices with their start and end apart: 2, of which 2 were waited for; matrix products, arithmetic and copies ran while one was open for 6% of the time, Pallas kernels for 0%

commit v1 on v0

v1 whole, which is shorter than its diff:
```python
import functools

import jax
import jax.numpy as jnp
from jax import lax
from jax.experimental import pallas as pl
from jax.experimental.pallas import tpu as pltpu
from jax.sharding import PartitionSpec as P

SOFT_CAP = 30.0
EXP2_SCALE = 30.0 * 1.4426950408889634
VMEM = pltpu.VMEM
PARAMS = pltpu.CompilerParams(vmem_limit_bytes=62 * 1024 * 1024)


def logits_kernel(x_ref, et_ref, t_ref, z_ref, *, sub):
    rows, cols = t_ref.shape
    here = pl.ds(pl.multiple_of(pl.program_id(1) * rows, rows), rows)

    @pl.when(pl.program_id(0) == 0)
    def _():
        z_ref[here, :] = jnp.zeros((rows, 128), jnp.float32)

    acc = jnp.zeros((rows, 128), jnp.float32)
    for s in range(cols // sub):
        z = jnp.dot(x_ref[...], et_ref[:, s * sub:(s + 1) * sub], preferred_element_type=jnp.float32)
        t = jnp.tanh(z * (1.0 / SOFT_CAP))
        t_ref[:, s * sub:(s + 1) * sub] = t
        e = jnp.exp2(t * EXP2_SCALE)
        for c in range(sub // 128):
            acc = acc + e[:, c * 128:(c + 1) * 128]
    z_ref[here, :] += acc


def logits_call(x, et, vb=1024, sub=1024, tb=512):
    tokens, dim = x.shape
    vocab = et.shape[1]
    return pl.pallas_call(
        functools.partial(logits_kernel, sub=sub),
        grid=(vocab // vb, tokens // tb),
        in_specs=[pl.BlockSpec((tb, dim), lambda v, t: (t, 0)), pl.BlockSpec((dim, vb), lambda v, t: (0, v))],
        out_specs=[pl.BlockSpec((tb, vb), lambda v, t: (t, v)), pl.BlockSpec((tokens, 128), lambda v, t: (0, 0))],
        out_shape=[jax.ShapeDtypeStruct((tokens, vocab), jnp.float32), jax.ShapeDtypeStruct((tokens, 128), jnp.float32)],
        compiler_params=PARAMS,
        cost_estimate=pl.CostEstimate(flops=2 * tokens * vocab * dim, bytes_accessed=4 * tokens * vocab, transcendentals=0),
        name="logits",
    )(x, et)


def grad_of(t, cz, a, lab, v0):
    e = jnp.exp2(t * EXP2_SCALE)
    vid = lax.broadcasted_iota(jnp.int32, t.shape, 1) + v0
    return ((e * cz - jnp.where(vid == lab, a, 0.0)) * (1.0 - t * t)).astype(jnp.bfloat16)


def gx_kernel(t_ref, et_ref, cz_ref, a_ref, lab_ref, g_ref, gx_ref, pick_ref, *, sub):
    vb = pl.program_id(1)

    @pl.when(vb == 0)
    def _():
        gx_ref[...] = jnp.zeros_like(gx_ref)
        pick_ref[...] = jnp.zeros_like(pick_ref)

    rows, cols = t_ref.shape
    pick = jnp.zeros((rows, 128), jnp.float32)
    for s in range(cols // sub):
        sl = slice(s * sub, (s + 1) * sub)
        v0 = vb * cols + s * sub
        t = t_ref[:, sl]
        g_ref[:, sl] = grad_of(t, cz_ref[...], a_ref[...], lab_ref[...], v0)
        hit = lax.broadcasted_iota(jnp.int32, t.shape, 1) + v0 == lab_ref[...]
        p = jnp.where(hit, t, 0.0)
        for c in range(sub // 128):
            pick = pick + p[:, c * 128:(c + 1) * 128]
    pick_ref[...] += pick
    gx_ref[...] += lax.dot_general(et_ref[...], g_ref[...], (((1,), (1,)), ((), ())), preferred_element_type=jnp.float32)


def gx_call(t, et, cz, a, lab, vb=1024, sub=256, tb=512):
    tokens, vocab = t.shape
    dim = et.shape[0]
    return pl.pallas_call(
        functools.partial(gx_kernel, sub=sub),
        grid=(tokens // tb, vocab // vb),
        in_specs=[pl.BlockSpec((tb, vb), lambda t, v: (t, v)), pl.BlockSpec((dim, vb), lambda t, v: (0, v))]
        + [pl.BlockSpec((tb, 1), lambda t, v: (t, 0))] * 3,
        out_specs=[pl.BlockSpec((tb, vb), lambda t, v: (t, v)), pl.BlockSpec((dim, tb), lambda t, v: (0, t)), pl.BlockSpec((tb, 128), lambda t, v: (t, 0))],
        out_shape=[jax.ShapeDtypeStruct((tokens, vocab), jnp.bfloat16), jax.ShapeDtypeStruct((dim, tokens), jnp.float32), jax.ShapeDtypeStruct((tokens, 128), jnp.float32)],
        compiler_params=PARAMS,
        cost_estimate=pl.CostEstimate(flops=2 * tokens * vocab * dim, bytes_accessed=6 * tokens * vocab, transcendentals=0),
        name="grad_x",
    )(t, et, cz, a, lab)


def table_kernel(go_ref, t_ref, xo_ref, xt_ref, cz_ref, a_ref, lab_ref, de_ref, gs_ref, *, sub):
    rows, cols = t_ref.shape
    v0 = pl.program_id(0) * cols
    for s in range(rows // sub):
        sl = slice(s * sub, (s + 1) * sub)
        gs_ref[sl, :] = grad_of(t_ref[sl, :], cz_ref[sl, :], a_ref[sl, :], lab_ref[sl, :], v0)
    own = jnp.dot(xo_ref[...], go_ref[...], preferred_element_type=jnp.float32)
    de_ref[...] = own + jnp.dot(xt_ref[...], gs_ref[...], preferred_element_type=jnp.float32)


def table_call(g_own, t_other, xt_own, xt_other, cz, a, lab, vb=512, sub=64):
    tokens, vocab = t_other.shape
    dim = xt_own.shape[0]
    whole = pl.BlockSpec(memory_space=VMEM)
    return pl.pallas_call(
        functools.partial(table_kernel, sub=sub),
        grid=(vocab // vb,),
        in_specs=[pl.BlockSpec((tokens, vb), lambda v: (0, v)), pl.BlockSpec((tokens, vb), lambda v: (0, v))] + [whole] * 5,
        out_specs=pl.BlockSpec((dim, vb), lambda v: (0, v)),
        out_shape=jax.ShapeDtypeStruct((dim, vocab), jnp.float32),
        scratch_shapes=[pltpu.VMEM((tokens, vb), jnp.bfloat16)],
        compiler_params=PARAMS,
        cost_estimate=pl.CostEstimate(flops=4 * tokens * vocab * dim, bytes_accessed=10 * tokens * vocab, transcendentals=0),
        name="grad_table",
    )(g_own, t_other, xt_own, xt_other, cz, a, lab)


def norm_kernel(h_ref, gain_ref, xf_ref, xb_ref, xr_ref):
    h = h_ref[0].astype(jnp.float32)
    inv = lax.rsqrt(jnp.mean(h * h, axis=0, keepdims=True) + 1e-6)
    xb = (h * inv * gain_ref[...]).astype(jnp.bfloat16)
    xb_ref[...] = xb
    xf_ref[...] = xb.astype(jnp.float32)
    xr_ref[...] = xb.T


def norm_call(ht, gain):
    batch, dim, seq = ht.shape
    return pl.pallas_call(
        norm_kernel,
        grid=(batch,),
        in_specs=[pl.BlockSpec((1, dim, seq), lambda b: (b, 0, 0)), pl.BlockSpec((dim, 1), lambda b: (0, 0))],
        out_specs=[pl.BlockSpec((dim, seq), lambda b: (0, b)), pl.BlockSpec((dim, seq), lambda b: (0, b)), pl.BlockSpec((seq, dim), lambda b: (b, 0))],
        out_shape=[jax.ShapeDtypeStruct((dim, batch * seq), jnp.float32), jax.ShapeDtypeStruct((dim, batch * seq), jnp.bfloat16), jax.ShapeDtypeStruct((batch * seq, dim), jnp.bfloat16)],
        compiler_params=PARAMS,
        name="norm",
    )(ht, gain)


def unpack_kernel(xf_ref, xb_ref, xr_ref):
    xb = xf_ref[...].astype(jnp.bfloat16)
    xb_ref[...] = xb
    xr_ref[...] = xb.T


def unpack_call(xf, seq=512):
    dim, tokens = xf.shape
    return pl.pallas_call(
        unpack_kernel,
        grid=(tokens // seq,),
        in_specs=[pl.BlockSpec((dim, seq), lambda b: (0, b))],
        out_specs=[pl.BlockSpec((dim, seq), lambda b: (0, b)), pl.BlockSpec((seq, dim), lambda b: (b, 0))],
        out_shape=[jax.ShapeDtypeStruct((dim, tokens), jnp.bfloat16), jax.ShapeDtypeStruct((tokens, dim), jnp.bfloat16)],
        compiler_params=PARAMS,
        name="unpack",
    )(xf)


def solution(mesh):
    n_tp = mesh.shape['tp']

    def local_step(hidden, norm_w, embed_table, labels, loss_mask):
        batch, seq, dim = hidden.shape
        vocab_local = embed_table.shape[0]
        tokens = batch * seq
        shard = dim // n_tp
        tp = lax.axis_index('tp')
        et = embed_table.T
        gain = (1.0 + norm_w.astype(jnp.float32))[:, None]
        ht = hidden.transpose(0, 2, 1).astype(jnp.float32)
        inv = lax.rsqrt(jnp.mean(ht * ht, axis=1, keepdims=True) + 1e-6)
        xf, xt, xr = norm_call(hidden.transpose(0, 2, 1), gain)
        mine = lax.dynamic_slice_in_dim(xf, tp * shard, shard, 0)
        other = lax.ppermute(mine, 'dp', [(0, 1), (1, 0)])
        xt_other, xr_other = unpack_call(lax.all_gather(other, 'tp', axis=0, tiled=True))
        lm = jnp.stack([labels.reshape(tokens), loss_mask.reshape(tokens)])
        lm_other = lax.ppermute(lm, 'dp', [(0, 1), (1, 0)])
        mask = lm[1].astype(jnp.float32)
        mask_other = lm_other[1].astype(jnp.float32)
        count = jnp.maximum(jnp.sum(mask) + jnp.sum(mask_other), 1.0)

        t_own, z_own = logits_call(xr, et)
        z_own = lax.psum(jnp.sum(z_own, axis=1), 'tp')
        a_own = mask / count
        g_own, gx, pick = gx_call(t_own, et, (a_own / z_own)[:, None], a_own[:, None], (lm[0] - tp * vocab_local)[:, None])
        t_other, z_other = logits_call(xr_other, et)
        gx = lax.psum(gx, 'tp')
        z_other = lax.psum(jnp.sum(z_other, axis=1), 'tp')
        a_other = mask_other / count
        grad_table = table_call(g_own, t_other, xt, xt_other, (a_other / z_other)[:, None], a_other[:, None], (lm_other[0] - tp * vocab_local)[:, None])

        picked = lax.psum(jnp.sum(pick, axis=1), 'tp') * SOFT_CAP
        loss = jnp.sum(mask * (jnp.log(z_own) - picked))
        gx3 = gx.reshape(dim, batch, seq).transpose(1, 0, 2)
        gg = gx3 * gain
        dot = jnp.sum(gg * ht, axis=1, keepdims=True)
        dh = (gg * inv - ht * (inv * inv * inv / dim) * dot).astype(hidden.dtype)
        dw = jnp.sum(gx3 * ht * inv, axis=(0, 2))
        loss, dw = lax.psum((loss, dw), 'dp')
        return loss / count, dh.transpose(0, 2, 1), dw, grad_table.T

    return jax.shard_map(local_step, mesh=mesh, in_specs=(P('dp', None, None), P(None), P('tp', None), P('dp', None), P('dp', None)), out_specs=(P(), P('dp', None, None), P(None), P('tp', None)), check_vma=False)
```

time: 816 us -> 402 us (0.49)
  waiting for transfers between devices: 563 us -> 118 us
  Pallas kernels: 0 us -> 179 us
  matrix products: 83.5 us -> 0 us
  other arithmetic: 69.1 us -> 15.6 us
  local copies, waits for them, and re-layouts: 34.5 us -> 23.8 us
    psum x2 -> x1, waiting for transfers between devices: 563 us -> 67.2 us  [local_step(): gx = lax.psum(gx, 'tp')]
    pallas_call x0 -> x6, Pallas kernels: none -> 179 us  [the longest x2 74.3 us: logits_call(): pl.pallas_call(functools.partial(logits_kernel, sub=sub), grid=(vocab //...]
    dot_general x3 -> x0, matrix products: 83.5 us -> none  [the longest x1 31.8 us: local_step(): jnp.einsum('td,vd->tv', normed_bf, embed_table, preferred_element_type=jn...]
    all_gather x0 -> x1, waiting for transfers between devices: none -> 34.1 us  [local_step(): lax.all_gather(other, 'tp', axis=0, tiled=True)]
    convert_element_type x3, other arithmetic: 35.5 us -> 3.5 us  [the longest x1 2.88 us: local_step(): dh = (gg * inv - ht * (inv * inv * inv / dim) * dot).astype(hidden.dtype)]
    reduce_sum x4 -> x7, other arithmetic: 33 us -> 10.7 us  [the longest x1 4.66 us: local_step(): dw = jnp.sum(gx3 * ht * inv, axis=(0, 2))]
    ppermute x0 -> x2, waiting for transfers between devices: none -> 16.1 us  [the longest x1 16.1 us: local_step(): other = lax.ppermute(mine, 'dp', [(0, 1), (1, 0)])]
    unnamed x10 -> x12, local copies, waits for them, and re-layouts: 19.4 us -> 3.81 us
  transfers between devices with their start and end apart: 2 -> 4, of which waited for: 2 -> 3; matrix products, arithmetic and copies ran while one was open for 6% -> 5% of each run, Pallas kernels for 0% -> 11%
where the time goes in v1:
time: 402 us; the launch traced here: 400 us
  Pallas kernels  179 us (45%)
  waiting for transfers between devices  118 us (29%)
  blocking collectives  42.8 us (11%)
  local copies, waits for them, and re-layouts  23.8 us (6%)
  between operations  17.3 us (4%)
  other arithmetic  15.6 us (4%)
  starting transfers between devices  4.13 us (1%)
    pallas_call x2, Pallas kernels, logits_call(): pl.pallas_call(functools.partial(logits_kernel, sub=sub), grid=(vocab //...  74.3 us
    psum x1, waiting for transfers between devices, local_step(): gx = lax.psum(gx, 'tp')  67.2 us
    pallas_call x1, Pallas kernels, table_call(): pl.pallas_call(functools.partial(table_kernel, sub=sub), grid=(vocab // v...  48.6 us
    pallas_call x1, Pallas kernels, gx_call(): pl.pallas_call(functools.partial(gx_kernel, sub=sub), grid=(tokens // tb,...  43.1 us
    all_gather x1, waiting for transfers between devices, local_step(): lax.all_gather(other, 'tp', axis=0, tiled=True)  34.1 us
    psum x1, blocking collectives, local_step(): picked = lax.psum(jnp.sum(pick, axis=1), 'tp') * SOFT_CAP  23.5 us
    ppermute x1, waiting for transfers between devices, local_step(): other = lax.ppermute(mine, 'dp', [(0, 1), (1, 0)])  16.1 us
    psum x1, blocking collectives, local_step(): z_own = lax.psum(jnp.sum(z_own, axis=1), 'tp')  13.6 us
  transfers between devices with their start and end apart: 4, of which 3 were waited for; matrix products, arithmetic and copies ran while one was open for 5% of the time, Pallas kernels for 11%

profile of v1, /device:TPU:0, one launch (start us, length us, event | category | flops | bytes accessed | tf_op | source)
XLA Modules:
  0.0 400.1 jit_solution(14516977296355926936)
XLA Ops:
  7.2 0.0 all-reduce.4.cloned.1.call-start
  7.2 0.7 copy.20
  7.9 0.7 copy.19
  8.6 3.3 collective-permute-start
  12.0 0.7 convert_add_fusion
  12.7 1.0 copy.10.gain_ref
  13.7 0.7 subtract_bitcast_fusion
  14.4 6.5 %norm.1 = (f32[960,1536]{1,0:T(8,128)}, bf16[960,1536]{1,0:T(8,128)(2,1)}, bf16[1536,960]{1,0:T(8,128)(2,1)}) custom-call(bf16[3,960,512]{2,1,0:T(8,128)(2,1)} %bitcast.37, f32[960,1]{1,0:T(8,128)} %copy.10.gain_ref), custom_call_target="tpu_custom_call" | custom-call | tf_op jit(solution)/shard_map/norm/pallas_call | solution.py:133
  20.9 0.0 copy-start.2
  20.9 37.1 %logits.2 = (f32[1536,6144]{1,0:T(8,128)}, f32[1536,128]{1,0:T(8,128)}) custom-call(bf16[1536,960]{1,0:T(8,128)(2,1)} %get-tuple-element.16.x_ref, bf16[960,6144]{1,0:T(8,128)(2,1)} %bitcast.48), custom_call_target="tpu_custom_call" | custom-call | flops 18119393280 | bytes 37748736 | tf_op jit(solution)/shard_map/logits/pallas_call | solution.py:38
  58.0 0.0 copy-done.2
  58.0 0.6 convert_reduce_fusion
  58.6 1.2 copy.24
  59.8 1.4 reduce_sum.81
  61.3 13.6 %psum.42 = f32[1536]{0:T(1024)S(1)} all-reduce(f32[1536]{0:T(1024)S(1)} %reduce_sum.81), channel_id=1, replica_groups=mesh['dp'=2,'tp'=8] {'tp'}, use_global_device_ids=true, to_apply=%region_1.0 | all-reduce | flops 1536 | bytes 12288 | tf_op jit(solution)/shard_map/psum | solution.py:187
  74.9 0.0 collective-permute-done
  74.9 0.6 fusion.7
  76.9 1.1 broadcast_in_dim.18.cz_ref
  78.0 1.2 copy.22
  79.2 43.1 %grad_x.1 = (bf16[1536,6144]{1,0:T(8,128)(2,1)}, f32[960,1536]{1,0:T(8,128)}, f32[1536,128]{1,0:T(8,128)}) custom-call(f32[1536,6144]{1,0:T(8,128)} %get-tuple-element.18.t_ref, bf16[960,6144]{1,0:T(8,128)(2,1)} %bitcast.49, f32[1536,1]{1,0:T(8,128)} %broadcast_in_dim.18.cz_ref, f32[1536,1]{1,0:T(8,128)} %bitcast.40, s32[1536,1]{1,0:T(8,128)} %bitcast.39), custom_call_target="tpu_custom_call" | custom-call | flops 18119393280 | bytes 56623104 | tf_op jit(solution)/shard_map/grad_x/pallas_call | solution.py:82
  122.3 6.4 %copy.14 = f32[960,1536]{0,1:T(8,128)} copy(f32[960,1536]{1,0:T(8,128)} %get-tuple-element.20) | data formatting | bytes 11796480 | tf_op jit(solution)/shard_map/grad_x/pallas_call | solution.py:82
  128.8 6.5 %copy.15 = f32[960,3,512]{2,0,1:T(8,128)} copy(f32[960,3,512]{0,2,1:T(8,128)} %bitcast.38) | data formatting | bytes 11796480 | tf_op jit(solution)/shard_map/reshape | solution.py:198
  135.3 0.0 copy-start
  135.3 0.0 all-reduce.4.cloned.1.call-update
  135.3 0.2 all-gather.2.cloned.1.call-start
  135.5 1.3 constant_dynamic-slice_fusion
  136.8 0.5 collective-permute-start.1
  137.4 16.1 %collective-permute-done.1 = f32[120,1536]{1,0:T(8,128)} collective-permute-done((f32[120,1536]{1,0:T(8,128)S(1)}, f32[120,1536]{1,0:T(8,128)}, u32[]{:S(2)}, u32[]{:S(2)}) %collective-permute-start.1) | collective-permute-done | bytes 737312 | tf_op jit(solution)/shard_map/ppermute | solution.py:178
  153.5 0.0 all-gather.2.cloned.1.call-update
  153.5 0.0 copy-done
  153.5 0.6 fusion
  154.2 1.4 reduce_sum.84
  155.6 1.2 copy.17.a_ref
  156.8 1.2 copy.18.lab_ref
  158.0 67.2 %all-reduce.4.cloned.1.call-done = f32[960,3,512]{2,0,1:T(8,128)} async-done(((f32[960,3,512]{2,0,1:T(8,128)}), f32[960,3,512]{2,0,1:T(8,128)}) %all-reduce.4.cloned.1.call-update) | async-done | bytes 5898256 | tf_op jit(solution)/shard_map/psum | solution.py:191
  225.2 0.0 copy-start.1
  225.2 4.7 %fusion.3 = (f32[960]{0:T(1024)S(1)}, f32[3,512]{1,0:T(4,128)S(1)}) fusion(f32[960,3,512]{2,0,1:T(8,128)} %all-reduce.4.cloned.1.call-done, f32[3,512]{1,0:T(4,128)S(1)} %get-tuple-element.37, bf16[3,512,960]{1,2,0:T(8,128)(2,1)S(1)} %copy-done, f32[960]{0:T(1024)S(1)} %convert_add_fusion), kind=kLoop, calls=%fused_computation.6 | loop fusion | flops 10319424 | bytes 8867328 | tf_op jit(solution)/shard_map/reduce_sum | solution.py:202
  229.9 0.0 copy-done.1
  229.9 2.9 fusion.4
  232.8 34.1 %all-gather.2.cloned.1.call-done.xf_ref = f32[960,1536]{1,0:T(8,128)} async-done(((f32[120,1536]{1,0:T(8,128)}), f32[960,1536]{1,0:T(8,128)}) %all-gather.2.cloned.1.call-update) | async-done | bytes 5898256 | tf_op jit(solution)/shard_map/all_gather | solution.py:179
  266.9 6.4 %unpack.1 = (bf16[960,1536]{1,0:T(8,128)(2,1)}, bf16[1536,960]{1,0:T(8,128)(2,1)}) custom-call(f32[960,1536]{1,0:T(8,128)} %all-gather.2.cloned.1.call-done.xf_ref), custom_call_target="tpu_custom_call" | custom-call | tf_op jit(solution)/shard_map/unpack/pallas_call | solution.py:152
  273.3 37.1 %logits.3 = (f32[1536,6144]{1,0:T(8,128)}, f32[1536,128]{1,0:T(8,128)}) custom-call(bf16[1536,960]{1,0:T(8,128)(2,1)} %get-tuple-element.23.x_ref, bf16[960,6144]{1,0:T(8,128)(2,1)} %bitcast.50), custom_call_target="tpu_custom_call" | custom-call | flops 18119393280 | bytes 37748736 | tf_op jit(solution)/shard_map/logits/pallas_call | solution.py:38
  310.5 1.4 reduce_sum.89
  311.9 23.5 %all-reduce = (f32[1536]{0:T(1024)S(1)}, f32[1536]{0:T(1024)S(1)}) all-reduce(f32[1536]{0:T(1024)S(1)} %reduce_sum.84, f32[1536]{0:T(1024)S(1)} %reduce_sum.89), channel_id=1, replica_groups=mesh['dp'=2,'tp'=8] {'tp'}, use_global_device_ids=true, to_apply=%region_5.0 | all-reduce | flops 3072 | bytes 24576 | tf_op jit(solution)/shard_map/psum | solution.py:196
  335.4 0.6 multiply_reduce_fusion
  336.0 5.7 %all-reduce.1 = (f32[]{:T(128)}, f32[960]{0:T(1024)}) all-reduce(f32[]{:T(128)} %multiply_reduce_fusion, f32[960]{0:T(1024)S(1)} %get-tuple-element.28), channel_id=1, replica_groups=mesh['dp'=2,'tp'=8] {'dp'}, use_global_device_ids=true, to_apply=%region_7.0 | all-reduce | flops 961 | bytes 7688 | tf_op jit(solution)/shard_map/psum | solution.py:203
  342.3 1.2 broadcast_in_dim.19.cz_ref
  343.5 48.6 %grad_table.1 = f32[960,6144]{1,0:T(8,128)} custom-call(bf16[1536,6144]{1,0:T(8,128)(2,1)} %get-tuple-element.21.go_ref, f32[1536,6144]{1,0:T(8,128)} %get-tuple-element.24.t_ref, bf16[960,1536]{1,0:T(8,128)(2,1)} %get-tuple-element.25.xo_ref, bf16[960,1536]{1,0:T(8,128)(2,1)} %get-tuple-element.26.xt_ref, f32[1536,1]{1,0:T(8,128)} %broadcast_in_dim.19.cz_ref, ...), custom_call_target="tpu_custom_call" | custom-call | flops 36238786560 | bytes 94371840 | tf_op jit(solution)/shard_map/grad_table/pallas_call | solution.py:109
  (11 shorter events, 0.1 us)
Async XLA Ops:
  7.2 218.1 %all-reduce.4.cloned.1.call-start = ((), (), s32[]{:S(2)}) async-start(), calls=%async_computation | async-start | bytes 11796480 | tf_op jit(solution)/shard_map/psum | solution.py:191
  8.6 66.3 %collective-permute-start = (s32[2,1536]{1,0:T(2,128)S(1)}, s32[2,1536]{1,0:T(2,128)S(1)}, u32[]{:S(2)}, u32[]{:S(2)}) collective-permute-start(s32[2,1536]{1,0:T(2,128)S(1)} %pad_add_fusion), channel_id=1, source_target_pairs={{0,8},{8,0},{1,9},{9,1},{2,10},{10,2},{3,11},{11,3},{4,12},{12,4},... | collective-permute-start | bytes 36872 | tf_op jit(solution)/shard_map/ppermute | solution.py:181
  20.9 37.1 %copy-start.2 = (s32[3,512]{1,0:T(4,128)S(1)}, s32[3,512]{1,0:T(4,128)}, u32[]{:S(2)}) copy-start(s32[3,512]{1,0:T(4,128)} %param.9) | copy-start | bytes 18436
  135.3 18.3 %copy-start = (bf16[3,512,960]{1,2,0:T(8,128)(2,1)S(1)}, bf16[3,512,960]{1,2,0:T(8,128)(2,1)}, u32[]{:S(2)}) copy-start(bf16[3,512,960]{1,2,0:T(8,128)(2,1)} %param.5) | copy-start | bytes 8847364
  135.3 131.6 %all-gather.2.cloned.1.call-start = ((), (), s32[]{:S(2)}) async-start(), calls=%async_computation.1 | async-start | bytes 6635520 | tf_op jit(solution)/shard_map/all_gather | solution.py:179
  136.8 16.7 %collective-permute-start.1 = (f32[120,1536]{1,0:T(8,128)S(1)}, f32[120,1536]{1,0:T(8,128)}, u32[]{:S(2)}, u32[]{:S(2)}) collective-permute-start(f32[120,1536]{1,0:T(8,128)S(1)} %constant_dynamic-slice_fusion), channel_id=1, source_target_pairs={{0,8},{8,0},{1,9},{9,1},{2,10},{10,2},{3,11},{11,3},{4,12},{12,4},... | collective-permute-start | bytes 2211848 | tf_op jit(solution)/shard_map/ppermute | solution.py:178
  225.2 4.7 %copy-start.1 = (f32[960,3,512]{2,0,1:T(8,128)S(1)}, f32[960,3,512]{2,0,1:T(8,128)}, u32[]{:S(2)}) copy-start(f32[960,3,512]{2,0,1:T(8,128)} %all-reduce.4.cloned.1.call-done) | copy-start | bytes 17694724
Sparse Core Ops, SparseCore 0:
  135.4 89.7 all-reduce.3
  227.1 39.8 all-gather.1
